TPU v7x, 32 devices: a whole 2x2x4 slice. The times are simulated.
32 devices in a mesh: front: 8 (over y, x, core), sub: 4 (over z).
Axes of the slice: x: 2, y: 2, z: 4, core: 2. Of those that a mesh axis runs over, the one named last changes fastest.
Arguments:
- row_values: float32 [4096, 1024], P(('front', 'sub')), may hold values from -0.12 to 0.12
- front_of_row: int32 [4096, 1], P(('front', 'sub')), may hold values from 0 to 7; in each aligned block of 128 rows (0 to 127, 128 to 255, ...) at most 32 rows name the same one
- child_factors: float32 [16, 512, 512], P('front', 'sub'), as said below
- child_columns: int32 [16, 512], P('front'), may hold values from 0 to 1023, as said below
- damping: float32 [8, 1024], P('front'), may hold values from 0.5 to 2
Outputs:
- front_factor: float32 [8, 1024, 1024], P('front', 'sub')
Inputs may be any that keep to these rules, and one draw needn't show every extreme that they name: `front_of_row`: among the 128 rows of one device, at most 32 name the same front, and some device's block reaches this bound. `child_factors`: each block is upper triangular with a positive diagonal. `child_columns`: each row names 512 distinct columns.
All inputs are finite; a program needn't handle non-finite values.
Results may differ from a plain program's by a relative error of at most 0.0003.
Values sent between devices are 32-bit elements; how exact they have to be, the bound alone decides.
A program may use at most 64 MiB of HBM per device.

v0:
```python
import functools
import jax, jax.numpy as jnp
from jax import lax
from jax.experimental import pallas as pl
from jax.experimental.pallas import tpu as pltpu
from jax.sharding import PartitionSpec as P

NB = 128
LAG = 3
BF = jnp.bfloat16
F32 = jnp.float32


def split3(x):
    h = x.astype(BF)
    r = x - h.astype(F32)
    m = r.astype(BF)
    l = (r - m.astype(F32)).astype(BF)
    return h, m, l


def split2(x):
    h = x.astype(BF)
    return h, (x - h.astype(F32)).astype(BF)


def tdot(a, b):
    return lax.dot_general(a, b, (((0,), (0,)), ((), ())), preferred_element_type=F32)


def mm(a, b):
    return lax.dot_general(a, b, (((1,), (0,)), ((), ())), preferred_element_type=F32)


def factor_diag(m_ref, B, slot):
    for b in range(NB // B):
        lo = b * B
        slot(b)
        rows = m_ref[lo:lo + B, :]
        sub = lax.broadcasted_iota(jnp.int32, (B, 1), 0)
        cs = [jnp.broadcast_to(rows[:, lo + j:lo + j + 1], (B, NB)) for j in range(B)]
        for j in range(B):
            c = cs[j]
            r = lax.rsqrt(c[j:j + 1, :])
            mult = jnp.where(sub > j, c * r, 0.0)
            r2 = jnp.concatenate([r, r], axis=1)
            pivot = rows[j:j + 1, :] * r2
            m2 = jnp.concatenate([mult, mult], axis=1)
            rows = jnp.where(sub == j, pivot, rows - m2 * pivot)
            for i in range(j + 1, B):
                cs[i] = cs[i] - mult * (cs[i][j:j + 1, :] * r)
        m_ref[lo:lo + B, :] = rows
        if lo + B < NB:
            h, m, l = split3(rows)
            left = jnp.concatenate([h, h, m, h, l, m], axis=0)[:, :NB]
            right = jnp.concatenate([h, m, h, l, h, m], axis=0)
            upd = tdot(left, right)
            m_ref[lo + B:, :] = m_ref[lo + B:, :] - upd[lo + B:, :]


MESH = pl.DeviceIdType.MESH


def fused_body(n, fronts, cap, B, x_ref, d_ref, ch_ref, cc_ref, w_ref, o_ref, out_ref, in_ref, fs, fg, a_ref, m_ref, rl_ref, rr_ref, xl_ref, xr_ref, p_ref, l_ref, r_ref, fr_ref, fl_ref, sr, sl, gl, gr):
    R, F = x_ref.shape
    kids, crows, _ = ch_ref.shape
    slots = fronts * cap
    K = kids * crows + slots
    panels = F // NB
    per = panels // n
    me = lax.axis_index("sub")
    right, left = lax.rem(me + 1, n), lax.rem(me + n - 1, n)
    first, last = me == 0, me == n - 1

    mine = lax.axis_index("front")
    barrier = pltpu.get_barrier_semaphore()
    for peer in (left, right):
        pl.semaphore_signal(barrier, inc=1, device_id={"sub": peer}, device_id_type=MESH)

    def greet(k, c):
        pl.semaphore_signal(barrier, inc=1, device_id={"front": lax.rem(mine + k, fronts)}, device_id_type=MESH)
        return c

    lax.fori_loop(1, fronts, greet, 0)

    dest = d_ref[...]
    hot = dest == lax.broadcasted_iota(jnp.int32, (R, fronts), 1)
    below = lax.broadcasted_iota(jnp.int32, (R, R), 1) < lax.broadcasted_iota(jnp.int32, (R, R), 0)
    before = mm(below.astype(F32).astype(BF), hot.astype(F32).astype(BF))
    position = jnp.sum(jnp.where(hot, before, 0.0), axis=1, keepdims=True)
    slot_of = dest.astype(F32) * cap + position
    pick = (slot_of == lax.broadcasted_iota(jnp.int32, (R, slots), 1).astype(F32)).astype(F32).astype(BF)
    out_ref[...] = tdot(jnp.concatenate([pick] * 3, axis=0), jnp.concatenate(split3(x_ref[...]), axis=0))
    pl.semaphore_wait(barrier, fronts + 1)

    def rows_of(f):
        return pl.ds(pl.multiple_of(f * cap, cap), cap)

    def post(k, dst_front):
        to = lax.rem(mine + k, fronts)
        return pltpu.make_async_remote_copy(
            src_ref=out_ref.at[rows_of(to)], dst_ref=in_ref.at[rows_of(dst_front)], send_sem=fs.at[k],
            recv_sem=fg.at[k], device_id={"front": to}, device_id_type=MESH)

    def post_rows(k, c):
        post(k, mine).start()
        return c

    lax.fori_loop(1, fronts, post_rows, 0)
    in_ref[rows_of(mine), :] = out_ref[rows_of(mine), :]

    def keep(start, count, h, l):
        for ref, parts in ((xr_ref, (h, l, h)), (xl_ref, (h, h, l))):
            for t, part in enumerate(parts):
                ref[t * K + start:t * K + start + count, :] = part

    for kid in range(kids):
        h, l = split2(ch_ref[kid])
        spread = (lax.broadcasted_iota(jnp.int32, (F, cc_ref.shape[1]), 0) == cc_ref[kid:kid + 1, :]).astype(F32).astype(BF)
        both = lax.dot_general(jnp.concatenate([h, l], axis=0), spread, (((1,), (1,)), ((), ())), preferred_element_type=F32)
        keep(kid * crows, crows, both[:crows].astype(BF), both[crows:].astype(BF))

    def take(k, c):
        post(k, lax.rem(mine + fronts - k, fronts)).wait_recv()
        return c

    lax.fori_loop(1, fronts, take, 0)
    h, l = split2(in_ref[...])
    keep(kids * crows, slots, h, l)

    ri = lax.broadcasted_iota(jnp.int32, (NB, NB), 0)
    ci = lax.broadcasted_iota(jnp.int32, (NB, NB), 1)

    def at(i, j):
        return (pl.ds(pl.multiple_of(i * NB, NB), NB), pl.ds(pl.multiple_of(j * NB, NB), NB))

    total = panels * (panels + 1) // 2
    ahead_left, ahead_right = LAG * (n - 1 - me), LAG * me

    def place(i, j):
        return i * panels - i * (i - 1) // 2 + j - i

    def to_right(src, c):
        return pltpu.make_async_remote_copy(
            src_ref=src.at[c], dst_ref=l_ref.at[c], send_sem=sr.at[c], recv_sem=gl.at[c],
            device_id={"sub": right}, device_id_type=MESH)

    def to_left(src, c):
        return pltpu.make_async_remote_copy(
            src_ref=src.at[c], dst_ref=r_ref.at[c], send_sem=sl.at[c], recv_sem=gr.at[c],
            device_id={"sub": left}, device_id_type=MESH)

    WB = 2 * NB

    def gram_row(i, carry):
        lt = xl_ref[:, pl.ds(pl.multiple_of(i * WB, WB), WB)].T

        def gram_col(j, c):
            block = mm(lt, xr_ref[:, pl.ds(pl.multiple_of(j * WB, WB), WB)])
            p_ref[place(2 * i, 2 * j)] = block[:NB, :NB]
            p_ref[place(2 * i, 2 * j + 1)] = block[:NB, NB:]
            p_ref[place(2 * i + 1, 2 * j + 1)] = block[NB:, NB:]

            @pl.when(j > i)
            def _():
                p_ref[place(2 * i + 1, 2 * j)] = block[NB:, :NB]
            return c

        lax.fori_loop(i, panels // 2, gram_col, 0)

        def launch(c, cc):
            @pl.when(first)
            def _():
                to_right(p_ref, c).start()

            @pl.when(last)
            def _():
                to_left(p_ref, c).start()
            return cc

        return lax.fori_loop(place(2 * i, 2 * i), place(2 * i + 2, 2 * i + 2), launch, carry)

    lax.fori_loop(0, panels // 2, gram_row, 0)

    def from_left(c):
        @pl.when((me > 0) & (c >= 0) & (c < total))
        def _():
            to_right(fr_ref, c).wait_recv()

            @pl.when(me < n - 1)
            def _():
                fr_ref[c] = l_ref[c] + p_ref[c]
                to_right(fr_ref, c).start()

    def from_right(c):
        @pl.when((me < n - 1) & (c >= 0) & (c < total))
        def _():
            to_left(fl_ref, c).wait_recv()

            @pl.when(me > 0)
            def _():
                fl_ref[c] = r_ref[c] + p_ref[c]
                to_left(fl_ref, c).start()

    def pass_on(q):
        from_left(q + ahead_left)
        from_right(q + ahead_right)

    def serve(i, j):
        c = place(i, j)
        pass_on(c)

        @pl.when(first)
        def _():
            a_ref[at(i, j)] = p_ref[c] + r_ref[c]

        @pl.when(last)
        def _():
            a_ref[at(i, j)] = p_ref[c] + l_ref[c]

        @pl.when((me > 0) & (me < n - 1))
        def _():
            a_ref[at(i, j)] = fr_ref[c] + r_ref[c]

        @pl.when(i == j)
        def _():
            wt = w_ref[:, pl.ds(pl.multiple_of(i * NB, NB), NB)]
            a_ref[at(i, j)] += jnp.where(ri == ci, wt * wt, 0.0)

    def fill(t, c):
        pass_on(t - LAG * (n - 1))
        return c

    lax.fori_loop(0, LAG * (n - 1), fill, 0)

    def first_row(j, c):
        serve(0, j)
        return c

    lax.fori_loop(0, panels, first_row, 0)

    def panel(p, carry):
        m_ref[:, :NB] = a_ref[at(p, p)]
        m_ref[:, NB:] = (ri == ci).astype(F32)

        def slot(k):
            @pl.when(p + 1 + k < panels)
            def _():
                serve(p + 1, p + 1 + k)

        factor_diag(m_ref, B, slot)

        def rest(k, c):
            @pl.when(p + 1 + k < panels)
            def _():
                serve(p + 1, p + 1 + k)
            return c

        lax.fori_loop(NB // B, max(NB // B, panels - 1), rest, 0)
        th, tl = split2(jnp.where(ci <= ri, m_ref[:, NB:], 0.0))
        tcat = jnp.concatenate([th, th, tl], axis=1)

        def cols(j, c):
            j0 = pl.multiple_of(j * NB, NB)
            h, l = split2(a_ref[at(p, j)])
            r = mm(tcat, jnp.concatenate([h, l, h], axis=0))
            a_ref[at(p, j)] = r
            h, l = split2(r)
            rl_ref[p, :, pl.ds(j0, NB)] = jnp.concatenate([h, h, l], axis=0)
            rr_ref[p, :, pl.ds(j0, NB)] = jnp.concatenate([h, l, h], axis=0)
            return c

        lax.fori_loop(p + 1, panels, cols, 0)
        a_ref[at(p, p)] = jnp.where(ci >= ri, m_ref[:, :NB], 0.0)

        @pl.when(p // per == me)
        def _():
            off = p - me * per

            def put(j, c):
                o_ref[at(off, j)] = jnp.where(j >= p, a_ref[at(p, j)], 0.0)
                return c
            lax.fori_loop(0, panels, put, 0)

        @pl.when(p + 1 < panels)
        def _():
            def term(q, c):
                lt = rl_ref[q, :, pl.ds(pl.multiple_of((p + 1) * NB, NB), NB)].T

                def inner(j, cc):
                    a_ref[at(p + 1, j)] -= mm(lt, rr_ref[q, :, pl.ds(pl.multiple_of(j * NB, NB), NB)])
                    return cc
                return lax.fori_loop(p + 1, panels, inner, c)
            lax.fori_loop(0, p + 1, term, 0)
        return carry

    lax.fori_loop(0, panels, panel, 0)

    def drain(c, carry):
        @pl.when(me < n - 1)
        def _():
            to_right(fr_ref, c).wait_send()

        @pl.when(me > 0)
        def _():
            to_left(fl_ref, c).wait_send()
        return carry

    lax.fori_loop(0, total, drain, 0)

    def sent(k, c):
        post(k, mine).wait_send()
        return c

    lax.fori_loop(1, fronts, sent, 0)


def local(row_values, front_of_row, child_factors, child_columns, damping, B=16):
    fronts, n = lax.axis_size("front"), lax.axis_size("sub")
    rows_held, F = row_values.shape
    cap = -(-(2 * rows_held // fronts) // 8) * 8
    K = fronts * cap + child_factors.shape[0] * child_factors.shape[1]
    panels = F // NB
    total = panels * (panels + 1) // 2
    sems = pltpu.SemaphoreType.DMA((total,))
    return pl.pallas_call(
        functools.partial(fused_body, n, fronts, cap, B),
        out_shape=jax.ShapeDtypeStruct((F // n, F), F32),
        in_specs=[pl.BlockSpec(memory_space=pltpu.VMEM)] * 5,
        out_specs=pl.BlockSpec(memory_space=pltpu.VMEM),
        scratch_shapes=[
            pltpu.VMEM((fronts * cap, F), F32),
            pltpu.VMEM((fronts * cap, F), F32),
            pltpu.SemaphoreType.DMA((fronts,)),
            pltpu.SemaphoreType.DMA((fronts,)),
            pltpu.VMEM((F, F), F32),
            pltpu.VMEM((NB, 2 * NB), F32),
            pltpu.VMEM((panels, 3 * NB, F), BF),
            pltpu.VMEM((panels, 3 * NB, F), BF),
            pltpu.VMEM((3 * K, F), BF),
            pltpu.VMEM((3 * K, F), BF),
        ] + [pltpu.VMEM((total, NB, NB), F32)] * 5 + [sems] * 4,
        compiler_params=pltpu.CompilerParams(
            vmem_limit_bytes=60 << 20, collective_id=0, has_side_effects=True),
        name="merge",
    )(row_values, front_of_row, child_factors, child_columns, damping)[None]


def solution(mesh):
    in_specs = (
        P(("front", "sub"), None),
        P(("front", "sub"), None),
        P("front", "sub", None),
        P("front", None),
        P("front", None),
    )
    out_specs = P("front", "sub", None)
    return jax.shard_map(local, mesh=mesh, in_specs=in_specs, out_specs=out_specs, check_vma=False)
```

profile of v0, /device:TPU:1, one launch (start us, length us, event | category | flops | bytes accessed | tf_op | source)
XLA Modules:
  0.0 116.5 jit_solution(3666220201156367589)
XLA Ops:
  0.0 1.4 %copy.6.d_ref = s32[128,1]{1,0:T(8,128)} copy(s32[128,1]{0,1:T(1,128)} %param.6) | data formatting | bytes 1024 | tf_op args[1]
  1.4 112.8 %merge.1 = f32[256,1024]{1,0:T(8,128)} custom-call(f32[128,1024]{1,0:T(8,128)} %x_ref.1, s32[128,1]{1,0:T(8,128)} %copy.6.d_ref, f32[2,128,512]{2,1,0:T(8,128)} %ch_ref.1, s32[2,512]{1,0:T(2,128)} %cc_ref.1, f32[1,1024]{1,0:T(1,128)} %w_ref.1), custom_call_target="tpu_custom_call" | custom-call | tf_op jit(solution)/shard_map/merge/pallas_call | solution.py:326
  114.2 2.3 %copy.8 = f32[1,256,1024]{2,1,0:T(8,128)} copy(f32[1,256,1024]{2,1,0:T(8,128)} %bitcast.1) | data formatting | bytes 2097152
where the time goes:
time: 117 us
  Pallas kernels  113 us (97%)
  local copies, waits for them, and re-layouts  3.7 us (3%)
    pallas_call x1, Pallas kernels, local(): pl.pallas_call(functools.partial(fused_body, n, fronts, cap, B), out_shap...  113 us
    unnamed x2, local copies, waits for them, and re-layouts  3.7 us

commit v1 on v0

v1 whole, which is shorter than its diff:
```python
import functools
import jax, jax.numpy as jnp
from jax import lax
from jax.experimental import pallas as pl
from jax.experimental.pallas import tpu as pltpu
from jax.sharding import PartitionSpec as P

NB = 128
CW = 2 * NB
BF = jnp.bfloat16
F32 = jnp.float32


def split3(x):
    h = x.astype(BF)
    r = x - h.astype(F32)
    m = r.astype(BF)
    l = (r - m.astype(F32)).astype(BF)
    return h, m, l


def split2(x):
    h = x.astype(BF)
    return h, (x - h.astype(F32)).astype(BF)


def tdot(a, b):
    return lax.dot_general(a, b, (((0,), (0,)), ((), ())), preferred_element_type=F32)


def mm(a, b):
    return lax.dot_general(a, b, (((1,), (0,)), ((), ())), preferred_element_type=F32)


def factor_diag(m_ref, B, slot):
    for b in range(NB // B):
        lo = b * B
        slot(b)
        rows = m_ref[lo:lo + B, :]
        sub = lax.broadcasted_iota(jnp.int32, (B, 1), 0)
        cs = [jnp.broadcast_to(rows[:, lo + j:lo + j + 1], (B, NB)) for j in range(B)]
        for j in range(B):
            c = cs[j]
            r = lax.rsqrt(c[j:j + 1, :])
            mult = jnp.where(sub > j, c * r, 0.0)
            r2 = jnp.concatenate([r, r], axis=1)
            pivot = rows[j:j + 1, :] * r2
            m2 = jnp.concatenate([mult, mult], axis=1)
            rows = jnp.where(sub == j, pivot, rows - m2 * pivot)
            for i in range(j + 1, B):
                cs[i] = cs[i] - mult * (cs[i][j:j + 1, :] * r)
        m_ref[lo:lo + B, :] = rows
        if lo + B < NB:
            h, m, l = split3(rows)
            left = jnp.concatenate([h, h, m, h, l, m], axis=0)[:, :NB]
            right = jnp.concatenate([h, m, h, l, h, m], axis=0)
            upd = tdot(left, right)
            m_ref[lo + B:, :] = m_ref[lo + B:, :] - upd[lo + B:, :]


MESH = pl.DeviceIdType.MESH


def dot3(lhs, h, l):
    return mm(lhs, jnp.concatenate([h, l, h], axis=0))


def left3(h, l):
    return jnp.concatenate([h, h, l], axis=1)


def fused_body(n, fronts, cap, B, x_ref, d_ref, ch_ref, cc_ref, w_ref, o_ref, out_ref, in_ref, fs, fg, a_ref, m_ref, rt_ref, rr_ref, tt_ref, xh_ref, xl_ref, th_ref, tl_ref, p_ref, l_ref, f_ref, ss, sg, os, og):
    R, F = x_ref.shape
    kids, crows, _ = ch_ref.shape
    slots = fronts * cap
    panels = F // NB
    chunks = F // CW
    per = panels // n
    me = lax.axis_index("sub")
    mine = lax.axis_index("front")
    side = lax.rem(mine, 2)
    pos = me + side * (n - 1 - 2 * me)
    top = (n - 1) * (1 - side)
    step = 1 - 2 * side
    is_root = pos == n - 1
    is_first = pos == 0

    barrier = pltpu.get_barrier_semaphore()

    def greet_sub(k, c):
        pl.semaphore_signal(barrier, inc=1, device_id={"sub": lax.rem(me + k, n)}, device_id_type=MESH)
        return c

    def greet_front(k, c):
        pl.semaphore_signal(barrier, inc=1, device_id={"front": lax.rem(mine + k, fronts)}, device_id_type=MESH)
        return c

    lax.fori_loop(1, n, greet_sub, 0)
    lax.fori_loop(1, fronts, greet_front, 0)

    def cols_of(c):
        return pl.ds(pl.multiple_of(c * CW, CW), CW)

    def rows_of(f):
        return pl.ds(pl.multiple_of(f * cap, cap), cap)

    def post(k, c, dst_front):
        to = lax.rem(mine + k, fronts)
        return pltpu.make_async_remote_copy(
            src_ref=out_ref.at[c, rows_of(to)], dst_ref=in_ref.at[c, rows_of(dst_front)], send_sem=fs.at[c, k],
            recv_sem=fg.at[c, k], device_id={"front": to}, device_id_type=MESH)

    dest = d_ref[...]
    hot = dest == lax.broadcasted_iota(jnp.int32, (R, fronts), 1)
    below = lax.broadcasted_iota(jnp.int32, (R, R), 1) < lax.broadcasted_iota(jnp.int32, (R, R), 0)
    before = mm(below.astype(F32).astype(BF), hot.astype(F32).astype(BF))
    position = jnp.sum(jnp.where(hot, before, 0.0), axis=1, keepdims=True)
    slot_of = dest.astype(F32) * cap + position
    pick = (slot_of == lax.broadcasted_iota(jnp.int32, (R, slots), 1).astype(F32)).astype(F32).astype(BF)
    pick2 = jnp.concatenate([pick, pick], axis=0).T

    def route(c):
        out_ref[c] = mm(pick2, jnp.concatenate(split2(x_ref[:, cols_of(c)]), axis=0))

    def post_rows(c):
        def one(k, cc):
            post(k, c, mine).start()
            return cc

        lax.fori_loop(1, fronts, one, 0)
        in_ref[c, rows_of(mine), :] = out_ref[c, rows_of(mine), :]

    route(0)
    pl.semaphore_wait(barrier, fronts + n - 2)
    post_rows(0)

    def route_rest(c, cc):
        route(c)
        post_rows(c)
        return cc

    lax.fori_loop(1, chunks, route_rest, 0)

    def place_kids(c, cc):
        for kid in range(kids):
            h, l = split2(ch_ref[kid])
            spread = (lax.broadcasted_iota(jnp.int32, (CW, cc_ref.shape[1]), 0) + c * CW == cc_ref[kid:kid + 1, :]).astype(F32).astype(BF)
            both = lax.dot_general(jnp.concatenate([h, l], axis=0), spread, (((1,), (1,)), ((), ())), preferred_element_type=F32)
            xh_ref[c, kid * crows:(kid + 1) * crows, :] = both[:crows].astype(BF)
            xl_ref[c, kid * crows:(kid + 1) * crows, :] = both[crows:].astype(BF)
        return cc

    lax.fori_loop(0, chunks, place_kids, 0)

    def place(i, j):
        return j * (j + 1) // 2 + i

    def hop(src, c):
        return pltpu.make_async_remote_copy(
            src_ref=src.at[c], dst_ref=l_ref.at[c], send_sem=ss.at[c], recv_sem=sg.at[c],
            device_id={"sub": lax.rem(me + step + n, n)}, device_id_type=MESH)

    def stream(c):
        @pl.when(is_first)
        def _():
            hop(p_ref, c).start()

        @pl.when((pos > 0) & (pos < n - 1))
        def _():
            hop(f_ref, c).wait_recv()
            f_ref[c] = l_ref[c] + p_ref[c]
            hop(f_ref, c).start()

    def gram_chunk(J, carry):
        def take(k, cc):
            post(k, J, lax.rem(mine + fronts - k, fronts)).wait_recv()
            return cc

        lax.fori_loop(1, fronts, take, 0)
        h, l = split2(in_ref[J])
        xh_ref[J, kids * crows:, :] = h
        xl_ref[J, kids * crows:, :] = l
        th_ref[J] = xh_ref[J].T
        tl_ref[J] = xl_ref[J].T

        def gram_block(I, cc):
            block = dot3(left3(th_ref[I], tl_ref[I]), xh_ref[J], xl_ref[J])
            i, j = 2 * I, 2 * J
            p_ref[place(i, j)] = block[:NB, :NB]
            p_ref[place(i, j + 1)] = block[:NB, NB:]
            p_ref[place(i + 1, j + 1)] = block[NB:, NB:]

            @pl.when(J > I)
            def _():
                p_ref[place(i + 1, j)] = block[NB:, :NB]

            stream(place(i, j))
            stream(place(i, j + 1))

            @pl.when(J > I)
            def _():
                stream(place(i + 1, j))

            stream(place(i + 1, j + 1))
            return cc

        return lax.fori_loop(0, J + 1, gram_block, carry)

    lax.fori_loop(0, chunks, gram_chunk, 0)

    ri = lax.broadcasted_iota(jnp.int32, (NB, NB), 0)
    ci = lax.broadcasted_iota(jnp.int32, (NB, NB), 1)

    def at(i, j):
        return (pl.ds(pl.multiple_of(i * NB, NB), NB), pl.ds(pl.multiple_of(j * NB, NB), NB))

    def at2(i, j):
        return (pl.ds(pl.multiple_of(i * CW, CW), CW), pl.ds(pl.multiple_of(j * CW, CW), CW))

    def ship(i, j):
        c = place(i, j)
        owner = i // per
        return pltpu.make_async_remote_copy(
            src_ref=a_ref.at[at(i, j)], dst_ref=o_ref.at[at(i - owner * per, j)], send_sem=os.at[c], recv_sem=og.at[c],
            device_id={"sub": owner}, device_id_type=MESH)

    def emit(i, j):
        @pl.when(i // per == me)
        def _():
            o_ref[at(i - me * per, j)] = a_ref[at(i, j)]

        @pl.when(i // per != me)
        def _():
            ship(i, j).start()

    def serve(i, j):
        c = place(i, j)
        hop(p_ref, c).wait_recv()
        a_ref[at(i, j)] = p_ref[c] + l_ref[c]

        @pl.when(i == j)
        def _():
            wt = w_ref[:, pl.ds(pl.multiple_of(i * NB, NB), NB)]
            a_ref[at(i, j)] += jnp.where(ri == ci, wt * wt, 0.0)

    def factor(p):
        m_ref[:, :NB] = a_ref[at(p, p)]
        m_ref[:, NB:] = (ri == ci).astype(F32)
        factor_diag(m_ref, B, lambda b: None)
        a_ref[at(p, p)] = jnp.where(ci >= ri, m_ref[:, :NB], 0.0)
        emit(p, p)
        return jnp.where(ci <= ri, m_ref[:, NB:], 0.0)

    def keep_t(P, r0, c0, t):
        h, l = split2(t)
        tt_ref[P, r0:r0 + NB, c0:c0 + NB] = h
        tt_ref[P, r0:r0 + NB, CW + c0:CW + c0 + NB] = h
        tt_ref[P, r0:r0 + NB, 2 * CW + c0:2 * CW + c0 + NB] = l

    def supercolumn(P, carry):
        for j in (2 * P, 2 * P + 1):
            def col(i, cc):
                serve(i, j)
                return cc
            lax.fori_loop(0, j + 1, col, 0)
        a_ref[at(2 * P + 1, 2 * P)] = jnp.zeros((NB, NB), F32)

        def solve(Q, cc):
            h, l = split2(a_ref[at2(Q, P)])
            r = dot3(tt_ref[Q], h, l)
            a_ref[at2(Q, P)] = r
            for i in range(2):
                for j in range(2):
                    emit(2 * Q + i, 2 * P + j)
            h, l = split2(r)
            rr_ref[...] = jnp.concatenate([h, l, h], axis=0)
            rt_ref[Q, P] = left3(h.T, l.T)

            def update(I, c3):
                a_ref[at2(I, P)] -= mm(rt_ref[Q, I], rr_ref[...])
                return c3

            return lax.fori_loop(Q + 1, P + 1, update, cc)

        lax.fori_loop(0, P, solve, 0)

        p = 2 * P
        t0 = factor(p)
        h, l = split2(a_ref[at(p, p + 1)])
        th, tl = split2(t0)
        r = dot3(left3(th, tl), h, l)
        a_ref[at(p, p + 1)] = r
        emit(p, p + 1)
        h, l = split2(r)
        rl = left3(h.T, l.T)
        a_ref[at(p + 1, p + 1)] -= dot3(rl, h, l)
        keep_t(P, 0, 0, t0)
        keep_t(P, 0, NB, jnp.zeros((NB, NB), F32))
        m2 = dot3(rl, th, tl)
        rr_ref[:NB, :NB], rr_ref[NB:CW, :NB] = split2(m2)
        t1 = factor(p + 1)
        keep_t(P, NB, NB, t1)
        th, tl = split2(t1)
        keep_t(P, NB, 0, -dot3(left3(th, tl), rr_ref[:NB, :NB], rr_ref[NB:CW, :NB]))
        return carry

    def over_blocks(row_lo, row_hi, fn):
        def row(i, c):
            def one(j, cc):
                fn(i, j)
                return cc
            return lax.fori_loop(i, panels, one, c)
        lax.fori_loop(row_lo, row_hi, row, 0)

    def blank(i, c):
        def one(j, cc):
            o_ref[at(i, j)] = jnp.zeros((NB, NB), F32)
            return cc
        return lax.fori_loop(0, me * per + i, one, c)

    lax.fori_loop(0, per, blank, 0)

    @pl.when(is_root)
    def _():
        lax.fori_loop(0, chunks, supercolumn, 0)

        def sent(i, j):
            @pl.when(i // per != me)
            def _():
                ship(i, j).wait_send()
        over_blocks(0, panels, sent)

    @pl.when(jnp.logical_not(is_root))
    def _():
        over_blocks(me * per, me * per + per, lambda i, j: ship(i, j).wait_recv())

        def sent(c, cc):
            hop(f_ref, c).wait_send()
            return cc
        lax.fori_loop(0, panels * (panels + 1) // 2, sent, 0)

    def sent_rows(c, cc):
        def one(k, c3):
            post(k, c, mine).wait_send()
            return c3
        return lax.fori_loop(1, fronts, one, cc)

    lax.fori_loop(0, chunks, sent_rows, 0)


def local(row_values, front_of_row, child_factors, child_columns, damping, B=16):
    fronts, n = lax.axis_size("front"), lax.axis_size("sub")
    rows_held, F = row_values.shape
    cap = -(-(2 * rows_held // fronts) // 8) * 8
    K = fronts * cap + child_factors.shape[0] * child_factors.shape[1]
    panels, chunks = F // NB, F // CW
    total = panels * (panels + 1) // 2
    DMA = pltpu.SemaphoreType.DMA
    return pl.pallas_call(
        functools.partial(fused_body, n, fronts, cap, B),
        out_shape=jax.ShapeDtypeStruct((F // n, F), F32),
        in_specs=[pl.BlockSpec(memory_space=pltpu.VMEM)] * 5,
        out_specs=pl.BlockSpec(memory_space=pltpu.VMEM),
        scratch_shapes=[
            pltpu.VMEM((chunks, fronts * cap, CW), F32),
            pltpu.VMEM((chunks, fronts * cap, CW), F32),
            DMA((chunks, fronts)),
            DMA((chunks, fronts)),
            pltpu.VMEM((F, F), F32),
            pltpu.VMEM((NB, 2 * NB), F32),
            pltpu.VMEM((chunks, chunks, CW, 3 * CW), BF),
            pltpu.VMEM((3 * CW, CW), BF),
            pltpu.VMEM((chunks, CW, 3 * CW), BF),
            pltpu.VMEM((chunks, K, CW), BF),
            pltpu.VMEM((chunks, K, CW), BF),
            pltpu.VMEM((chunks, CW, K), BF),
            pltpu.VMEM((chunks, CW, K), BF),
        ] + [pltpu.VMEM((total, NB, NB), F32)] * 3 + [DMA((total,))] * 4,
        compiler_params=pltpu.CompilerParams(
            vmem_limit_bytes=60 << 20, collective_id=0, has_side_effects=True),
        name="merge",
    )(row_values, front_of_row, child_factors, child_columns, damping)[None]


def solution(mesh):
    in_specs = (
        P(("front", "sub"), None),
        P(("front", "sub"), None),
        P("front", "sub", None),
        P("front", None),
        P("front", None),
    )
    out_specs = P("front", "sub", None)
    return jax.shard_map(local, mesh=mesh, in_specs=in_specs, out_specs=out_specs, check_vma=False)
```

time: 117 us -> 78.9 us (0.67)
  Pallas kernels: 113 us -> 75 us
    pallas_call x1, Pallas kernels: 113 us -> 75 us  [local(): pl.pallas_call(functools.partial(fused_body, n, fronts, cap, B), out_shap...]
where the time goes in v1:
time: 78.9 us; the launch traced here: 78.7 us
  Pallas kernels  75 us (95%)
  local copies, waits for them, and re-layouts  3.7 us (5%)
    pallas_call x1, Pallas kernels, local(): pl.pallas_call(functools.partial(fused_body, n, fronts, cap, B), out_shap...  75 us
    unnamed x2, local copies, waits for them, and re-layouts  3.7 us

profile of v1, /device:TPU:1, one launch (start us, length us, event | category | flops | bytes accessed | tf_op | source)
XLA Modules:
  0.0 78.7 jit_solution(8368172829664043305)
XLA Ops:
  0.0 1.4 %copy.6.d_ref = s32[128,1]{1,0:T(8,128)} copy(s32[128,1]{0,1:T(1,128)} %param.6) | data formatting | bytes 1024 | tf_op args[1]
  1.4 75.0 %merge.1 = f32[256,1024]{1,0:T(8,128)} custom-call(f32[128,1024]{1,0:T(8,128)} %x_ref.1, s32[128,1]{1,0:T(8,128)} %copy.6.d_ref, f32[2,128,512]{2,1,0:T(8,128)} %ch_ref.1, s32[2,512]{1,0:T(2,128)} %cc_ref.1, f32[1,1024]{1,0:T(1,128)} %w_ref.1), custom_call_target="tpu_custom_call" | custom-call | tf_op jit(solution)/shard_map/merge/pallas_call | solution.py:359
  76.4 2.3 %copy.8 = f32[1,256,1024]{2,1,0:T(8,128)} copy(f32[1,256,1024]{2,1,0:T(8,128)} %bitcast.1) | data formatting | bytes 2097152

commit v2 on v1

--- a/solution.py
+++ b/solution.py
@@ -69,13 +69,12 @@
     return jnp.concatenate([h, h, l], axis=1)
 
 
-def fused_body(n, fronts, cap, B, x_ref, d_ref, ch_ref, cc_ref, w_ref, o_ref, out_ref, in_ref, fs, fg, a_ref, m_ref, rt_ref, rr_ref, tt_ref, xh_ref, xl_ref, th_ref, tl_ref, p_ref, l_ref, f_ref, ss, sg, os, og):
+def fused_body(n, fronts, cap, B, x_ref, d_ref, ch_ref, cc_ref, w_ref, o_ref, out_ref, in_ref, fs, fg, a_ref, m_ref, rt_ref, rr_ref, mh_ref, ml_ref, tt_ref, xh_ref, xl_ref, th_ref, tl_ref, p_ref, l_ref, f_ref, dp_ref, dl_ref, df_ref, dr_ref, rd_ref, ss, sg, ds, dg, os, og, ps, pg, go):
     R, F = x_ref.shape
     kids, crows, _ = ch_ref.shape
     slots = fronts * cap
     panels = F // NB
     chunks = F // CW
-    per = panels // n
     me = lax.axis_index("sub")
     mine = lax.axis_index("front")
     side = lax.rem(mine, 2)
@@ -111,13 +110,13 @@
             recv_sem=fg.at[c, k], device_id={"front": to}, device_id_type=MESH)
 
     dest = d_ref[...]
-    hot = dest == lax.broadcasted_iota(jnp.int32, (R, fronts), 1)
-    below = lax.broadcasted_iota(jnp.int32, (R, R), 1) < lax.broadcasted_iota(jnp.int32, (R, R), 0)
-    before = mm(below.astype(F32).astype(BF), hot.astype(F32).astype(BF))
-    position = jnp.sum(jnp.where(hot, before, 0.0), axis=1, keepdims=True)
+    hot = dest == lax.broadcasted_iota(jnp.int32, (fronts, R), 0)
+    above = lax.broadcasted_iota(jnp.int32, (R, R), 0) < lax.broadcasted_iota(jnp.int32, (R, R), 1)
+    before = mm(hot.astype(F32).astype(BF), above.astype(F32).astype(BF))
+    position = jnp.sum(jnp.where(hot, before, 0.0), axis=0, keepdims=True)
     slot_of = dest.astype(F32) * cap + position
-    pick = (slot_of == lax.broadcasted_iota(jnp.int32, (R, slots), 1).astype(F32)).astype(F32).astype(BF)
-    pick2 = jnp.concatenate([pick, pick], axis=0).T
+    pick = (slot_of == lax.broadcasted_iota(jnp.int32, (slots, R), 0).astype(F32)).astype(F32).astype(BF)
+    pick2 = jnp.concatenate([pick, pick], axis=1)
 
     def route(c):
         out_ref[c] = mm(pick2, jnp.concatenate(split2(x_ref[:, cols_of(c)]), axis=0))
@@ -152,24 +151,37 @@
 
     lax.fori_loop(0, chunks, place_kids, 0)
 
+    ri = lax.broadcasted_iota(jnp.int32, (NB, NB), 0)
+    ci = lax.broadcasted_iota(jnp.int32, (NB, NB), 1)
+
     def place(i, j):
         return j * (j + 1) // 2 + i
 
-    def hop(src, c):
+    def hop(src, dst, c, send, recv):
         return pltpu.make_async_remote_copy(
-            src_ref=src.at[c], dst_ref=l_ref.at[c], send_sem=ss.at[c], recv_sem=sg.at[c],
+            src_ref=src.at[c], dst_ref=dst.at[c], send_sem=send.at[c], recv_sem=recv.at[c],
             device_id={"sub": lax.rem(me + step + n, n)}, device_id_type=MESH)
 
-    def stream(c):
+    def hop_block(src, c):
+        return hop(src, l_ref, c, ss, sg)
+
+    def hop_pair(src, J):
+        return hop(src, dl_ref, J, ds, dg)
+
+    def stream(copy, own, came, sums, c):
         @pl.when(is_first)
         def _():
-            hop(p_ref, c).start()
+            copy(own, c).start()
 
         @pl.when((pos > 0) & (pos < n - 1))
         def _():
-            hop(f_ref, c).wait_recv()
-            f_ref[c] = l_ref[c] + p_ref[c]
-            hop(f_ref, c).start()
+            copy(sums, c).wait_recv()
+            sums[c] = came[c] + own[c]
+            copy(sums, c).start()
+
+    def pack(ref, c, a, b):
+        ref[c, :NB, :] = jnp.where(ci >= ri, a, b)
+        ref[c, NB:, :] = jnp.broadcast_to(jnp.sum(jnp.where(ri == ci, b, 0.0), axis=0, keepdims=True), (8, NB))
 
     def gram_chunk(J, carry):
         def take(k, cc):
@@ -186,30 +198,31 @@
         def gram_block(I, cc):
             block = dot3(left3(th_ref[I], tl_ref[I]), xh_ref[J], xl_ref[J])
             i, j = 2 * I, 2 * J
-            p_ref[place(i, j)] = block[:NB, :NB]
             p_ref[place(i, j + 1)] = block[:NB, NB:]
-            p_ref[place(i + 1, j + 1)] = block[NB:, NB:]
 
             @pl.when(J > I)
             def _():
+                p_ref[place(i, j)] = block[:NB, :NB]
                 p_ref[place(i + 1, j)] = block[NB:, :NB]
-
-            stream(place(i, j))
-            stream(place(i, j + 1))
+                p_ref[place(i + 1, j + 1)] = block[NB:, NB:]
+                stream(hop_block, p_ref, l_ref, f_ref, place(i, j))
+                stream(hop_block, p_ref, l_ref, f_ref, place(i + 1, j))
+
+            @pl.when(J == I)
+            def _():
+                pack(dp_ref, J, block[:NB, :NB], block[NB:, NB:])
+                stream(hop_pair, dp_ref, dl_ref, df_ref, J)
+
+            stream(hop_block, p_ref, l_ref, f_ref, place(i, j + 1))
 
             @pl.when(J > I)
             def _():
-                stream(place(i + 1, j))
-
-            stream(place(i + 1, j + 1))
+                stream(hop_block, p_ref, l_ref, f_ref, place(i + 1, j + 1))
             return cc
 
         return lax.fori_loop(0, J + 1, gram_block, carry)
 
     lax.fori_loop(0, chunks, gram_chunk, 0)
-
-    ri = lax.broadcasted_iota(jnp.int32, (NB, NB), 0)
-    ci = lax.broadcasted_iota(jnp.int32, (NB, NB), 1)
 
     def at(i, j):
         return (pl.ds(pl.multiple_of(i * NB, NB), NB), pl.ds(pl.multiple_of(j * NB, NB), NB))
@@ -217,38 +230,69 @@
     def at2(i, j):
         return (pl.ds(pl.multiple_of(i * CW, CW), CW), pl.ds(pl.multiple_of(j * CW, CW), CW))
 
-    def ship(i, j):
-        c = place(i, j)
-        owner = i // per
+    span = chunks // n
+
+    def ship(Q, P):
+        owner = Q // span
         return pltpu.make_async_remote_copy(
-            src_ref=a_ref.at[at(i, j)], dst_ref=o_ref.at[at(i - owner * per, j)], send_sem=os.at[c], recv_sem=og.at[c],
-            device_id={"sub": owner}, device_id_type=MESH)
-
-    def emit(i, j):
-        @pl.when(i // per == me)
-        def _():
-            o_ref[at(i - me * per, j)] = a_ref[at(i, j)]
-
-        @pl.when(i // per != me)
-        def _():
-            ship(i, j).start()
+            src_ref=a_ref.at[at2(Q, P)], dst_ref=o_ref.at[at2(Q - owner * span, P)], send_sem=os.at[Q, P],
+            recv_sem=og.at[Q, P], device_id={"sub": owner}, device_id_type=MESH)
+
+    def ship_side(P):
+        owner = P // span
+        return pltpu.make_async_remote_copy(
+            src_ref=a_ref.at[at(2 * P, 2 * P + 1)], dst_ref=o_ref.at[at(2 * (P - owner * span), 2 * P + 1)],
+            send_sem=os.at[P, P], recv_sem=og.at[P, P], device_id={"sub": owner}, device_id_type=MESH)
+
+    def ship_pair(P):
+        return pltpu.make_async_remote_copy(
+            src_ref=dr_ref.at[P], dst_ref=rd_ref.at[P], send_sem=ps.at[P], recv_sem=pg.at[P],
+            device_id={"sub": P // span}, device_id_type=MESH)
+
+    hold = chunks // 2
+
+    def send_column(P):
+        def one(Q, cc):
+            @pl.when(Q // span == me)
+            def _():
+                o_ref[at2(Q - me * span, P)] = a_ref[at2(Q, P)]
+
+            @pl.when(Q // span != me)
+            def _():
+                ship(Q, P).start()
+            return cc
+        lax.fori_loop(0, P, one, 0)
+
+    def send_side(P):
+        @pl.when(P // span != me)
+        def _():
+            ship_side(P).start()
+
+    def send_pair(P):
+        @pl.when(P // span != me)
+        def _():
+            ship_pair(P).start()
 
     def serve(i, j):
         c = place(i, j)
-        hop(p_ref, c).wait_recv()
+        hop_block(p_ref, c).wait_recv()
         a_ref[at(i, j)] = p_ref[c] + l_ref[c]
 
-        @pl.when(i == j)
-        def _():
+    def serve_pair(P):
+        hop_pair(dp_ref, P).wait_recv()
+        m = dp_ref[P, :NB, :] + dl_ref[P, :NB, :]
+        d = dp_ref[P, NB:, :] + dl_ref[P, NB:, :]
+        mt = m.T
+        for k, block in ((0, jnp.where(ci >= ri, m, mt)), (1, jnp.where(ci > ri, mt, jnp.where(ci < ri, m, d[:1])))):
+            i = 2 * P + k
             wt = w_ref[:, pl.ds(pl.multiple_of(i * NB, NB), NB)]
-            a_ref[at(i, j)] += jnp.where(ri == ci, wt * wt, 0.0)
+            a_ref[at(i, i)] = block + jnp.where(ri == ci, wt * wt, 0.0)
 
     def factor(p):
         m_ref[:, :NB] = a_ref[at(p, p)]
         m_ref[:, NB:] = (ri == ci).astype(F32)
         factor_diag(m_ref, B, lambda b: None)
         a_ref[at(p, p)] = jnp.where(ci >= ri, m_ref[:, :NB], 0.0)
-        emit(p, p)
         return jnp.where(ci <= ri, m_ref[:, NB:], 0.0)
 
     def keep_t(P, r0, c0, t):
@@ -258,86 +302,151 @@
         tt_ref[P, r0:r0 + NB, 2 * CW + c0:2 * CW + c0 + NB] = l
 
     def supercolumn(P, carry):
-        for j in (2 * P, 2 * P + 1):
-            def col(i, cc):
-                serve(i, j)
-                return cc
-            lax.fori_loop(0, j + 1, col, 0)
-        a_ref[at(2 * P + 1, 2 * P)] = jnp.zeros((NB, NB), F32)
-
-        def solve(Q, cc):
-            h, l = split2(a_ref[at2(Q, P)])
-            r = dot3(tt_ref[Q], h, l)
-            a_ref[at2(Q, P)] = r
+        def subtract(I, cc):
+            def one(Q, c3):
+                a_ref[at2(I, P)] -= mm(rt_ref[Q, I], rr_ref[Q])
+                return c3
+            return lax.fori_loop(0, I, one, cc)
+
+        def solve(I, cc):
             for i in range(2):
                 for j in range(2):
-                    emit(2 * Q + i, 2 * P + j)
+                    serve(2 * I + i, 2 * P + j)
+            subtract(I, cc)
+            h, l = split2(a_ref[at2(I, P)])
+            r = dot3(tt_ref[I], h, l)
+            a_ref[at2(I, P)] = r
             h, l = split2(r)
-            rr_ref[...] = jnp.concatenate([h, l, h], axis=0)
-            rt_ref[Q, P] = left3(h.T, l.T)
-
-            def update(I, c3):
-                a_ref[at2(I, P)] -= mm(rt_ref[Q, I], rr_ref[...])
-                return c3
-
-            return lax.fori_loop(Q + 1, P + 1, update, cc)
+            rr_ref[I] = jnp.concatenate([h, l, h], axis=0)
+            rt_ref[I, P] = left3(h.T, l.T)
+            return cc
 
         lax.fori_loop(0, P, solve, 0)
 
+        @pl.when(P == hold)
+        def _():
+            pl.semaphore_wait(go, 1)
+
+            def backlog(K, cc):
+                send_column(K)
+
+                @pl.when(K < P)
+                def _():
+                    send_side(K)
+                    send_pair(K)
+                return cc
+            lax.fori_loop(0, P + 1, backlog, 0)
+
+        @pl.when(P > hold)
+        def _():
+            send_column(P)
+
+        serve(2 * P, 2 * P + 1)
+        serve_pair(P)
+        a_ref[at(2 * P + 1, 2 * P)] = jnp.zeros((NB, NB), F32)
+        subtract(P, 0)
         p = 2 * P
         t0 = factor(p)
         h, l = split2(a_ref[at(p, p + 1)])
         th, tl = split2(t0)
         r = dot3(left3(th, tl), h, l)
         a_ref[at(p, p + 1)] = r
-        emit(p, p + 1)
+
+        @pl.when(P >= hold)
+        def _():
+            send_side(P)
+
         h, l = split2(r)
         rl = left3(h.T, l.T)
         a_ref[at(p + 1, p + 1)] -= dot3(rl, h, l)
         keep_t(P, 0, 0, t0)
         keep_t(P, 0, NB, jnp.zeros((NB, NB), F32))
-        m2 = dot3(rl, th, tl)
-        rr_ref[:NB, :NB], rr_ref[NB:CW, :NB] = split2(m2)
+        mh_ref[...], ml_ref[...] = split2(dot3(rl, th, tl))
         t1 = factor(p + 1)
+        a_ref[at(p + 1, p)] = jnp.zeros((NB, NB), F32)
+
+        @pl.when(P // span == me)
+        def _():
+            o_ref[at2(P - me * span, P)] = a_ref[at2(P, P)]
+
+        @pl.when(P // span != me)
+        def _():
+            pack(dr_ref, P, a_ref[at(p, p)], a_ref[at(p + 1, p + 1)].T)
+
+        @pl.when(P >= hold)
+        def _():
+            send_pair(P)
+
         keep_t(P, NB, NB, t1)
         th, tl = split2(t1)
-        keep_t(P, NB, 0, -dot3(left3(th, tl), rr_ref[:NB, :NB], rr_ref[NB:CW, :NB]))
+        keep_t(P, NB, 0, -dot3(left3(th, tl), mh_ref[...], ml_ref[...]))
         return carry
 
-    def over_blocks(row_lo, row_hi, fn):
-        def row(i, c):
-            def one(j, cc):
-                fn(i, j)
+    def over_blocks(lo, hi, fn, pair):
+        def row(Q, c):
+            def one(P, cc):
+                fn(Q, P)
                 return cc
-            return lax.fori_loop(i, panels, one, c)
-        lax.fori_loop(row_lo, row_hi, row, 0)
+            pair(Q)
+            return lax.fori_loop(Q + 1, chunks, one, c)
+        lax.fori_loop(lo, hi, row, 0)
 
     def blank(i, c):
         def one(j, cc):
-            o_ref[at(i, j)] = jnp.zeros((NB, NB), F32)
+            o_ref[at2(i, j)] = jnp.zeros((CW, CW), F32)
             return cc
-        return lax.fori_loop(0, me * per + i, one, c)
-
-    lax.fori_loop(0, per, blank, 0)
+        return lax.fori_loop(0, me * span + i, one, c)
+
+    lax.fori_loop(0, span, blank, 0)
 
     @pl.when(is_root)
     def _():
         lax.fori_loop(0, chunks, supercolumn, 0)
 
-        def sent(i, j):
-            @pl.when(i // per != me)
-            def _():
-                ship(i, j).wait_send()
-        over_blocks(0, panels, sent)
+        def sent(Q, P):
+            @pl.when(Q // span != me)
+            def _():
+                ship(Q, P).wait_send()
+
+        def sent_pair(P):
+            @pl.when(P // span != me)
+            def _():
+                ship_side(P).wait_send()
+                ship_pair(P).wait_send()
+
+        over_blocks(0, chunks, sent, sent_pair)
 
     @pl.when(jnp.logical_not(is_root))
     def _():
-        over_blocks(me * per, me * per + per, lambda i, j: ship(i, j).wait_recv())
-
         def sent(c, cc):
-            hop(f_ref, c).wait_send()
-            return cc
-        lax.fori_loop(0, panels * (panels + 1) // 2, sent, 0)
+            hop_pair(df_ref, c).wait_send()
+            hop_block(f_ref, place(2 * c, 2 * c + 1)).wait_send()
+
+            def off(i, c3):
+                hop_block(f_ref, place(i, 2 * c)).wait_send()
+                hop_block(f_ref, place(i, 2 * c + 1)).wait_send()
+                return c3
+            return lax.fori_loop(0, 2 * c, off, cc)
+        lax.fori_loop(0, chunks, sent, 0)
+
+        @pl.when(is_first)
+        def _():
+            pl.semaphore_signal(go, inc=1, device_id={"front": mine + 1 - 2 * side}, device_id_type=MESH)
+
+        def came(Q, P):
+            ship(Q, P).wait_recv()
+
+        def came_pair(P):
+            ship_side(P).wait_recv()
+            ship_pair(P).wait_recv()
+            k = 2 * (P - me * span)
+            m = rd_ref[P, :NB, :]
+            o_ref[at(k, 2 * P)] = jnp.where(ci >= ri, m, 0.0)
+            o_ref[at(k + 1, 2 * P)] = jnp.zeros((NB, NB), F32)
+            o_ref[at(k + 1, 2 * P + 1)] = jnp.where(ci > ri, m.T, jnp.where(ci == ri, rd_ref[P, NB:NB + 1, :], 0.0))
+
+        over_blocks(me * span, me * span + span, came, came_pair)
+
 
     def sent_rows(c, cc):
         def one(k, c3):
@@ -369,17 +478,20 @@
             pltpu.VMEM((F, F), F32),
             pltpu.VMEM((NB, 2 * NB), F32),
             pltpu.VMEM((chunks, chunks, CW, 3 * CW), BF),
-            pltpu.VMEM((3 * CW, CW), BF),
+            pltpu.VMEM((chunks, 3 * CW, CW), BF),
+            pltpu.VMEM((NB, NB), BF),
+            pltpu.VMEM((NB, NB), BF),
             pltpu.VMEM((chunks, CW, 3 * CW), BF),
             pltpu.VMEM((chunks, K, CW), BF),
             pltpu.VMEM((chunks, K, CW), BF),
             pltpu.VMEM((chunks, CW, K), BF),
             pltpu.VMEM((chunks, CW, K), BF),
-        ] + [pltpu.VMEM((total, NB, NB), F32)] * 3 + [DMA((total,))] * 4,
+        ] + [pltpu.VMEM((total, NB, NB), F32)] * 3 + [pltpu.VMEM((chunks, NB + 8, NB), F32)] * 5
+        + [DMA((total,))] * 2 + [DMA((chunks,))] * 2 + [DMA((chunks, chunks))] * 2 + [DMA((chunks,))] * 2 + [pltpu.SemaphoreType.REGULAR],
         compiler_params=pltpu.CompilerParams(
             vmem_limit_bytes=60 << 20, collective_id=0, has_side_effects=True),
         name="merge",
-    )(row_values, front_of_row, child_factors, child_columns, damping)[None]
+    )(row_values, front_of_row.reshape(1, rows_held), child_factors, child_columns, damping)[None]
 
 
 def solution(mesh):

time: 78.9 us -> 66.1 us (0.84)
  the two profiles are of different devices: /device:TPU:1 before, /device:TPU:16 now
where the time goes in v2:
time: 66.1 us; the launch traced here: 65.9 us
  Pallas kernels  63.6 us (96%)
  local copies, waits for them, and re-layouts  2.31 us (3%)
    pallas_call x1, Pallas kernels, local(): pl.pallas_call(functools.partial(fused_body, n, fronts, cap, B), out_shap...  63.6 us
    unnamed x1, local copies, waits for them, and re-layouts  2.31 us

profile of v2, /device:TPU:16, one launch (start us, length us, event | category | flops | bytes accessed | tf_op | source)
XLA Modules:
  0.0 65.9 jit_solution(14618187410827203749)
XLA Ops:
  0.0 63.6 %merge.1 = f32[256,1024]{1,0:T(8,128)} custom-call(f32[128,1024]{1,0:T(8,128)} %x_ref.1, s32[1,128]{1,0:T(1,128)} %bitcast.3, f32[2,128,512]{2,1,0:T(8,128)} %ch_ref.1, s32[2,512]{1,0:T(2,128)} %cc_ref.1, f32[1,1024]{1,0:T(1,128)} %w_ref.1), custom_call_target="tpu_custom_call" | custom-call | tf_op jit(solution)/shard_map/merge/pallas_call | solution.py:468
  63.6 2.3 %copy.7 = f32[1,256,1024]{2,1,0:T(8,128)} copy(f32[1,256,1024]{2,1,0:T(8,128)} %bitcast.2) | data formatting | bytes 2097152

commit v3 on v2

--- a/solution.py
+++ b/solution.py
@@ -11,51 +11,74 @@
 F32 = jnp.float32
 
 
-def split3(x):
-    h = x.astype(BF)
-    r = x - h.astype(F32)
-    m = r.astype(BF)
-    l = (r - m.astype(F32)).astype(BF)
-    return h, m, l
-
-
 def split2(x):
     h = x.astype(BF)
     return h, (x - h.astype(F32)).astype(BF)
 
 
-def tdot(a, b):
-    return lax.dot_general(a, b, (((0,), (0,)), ((), ())), preferred_element_type=F32)
-
-
 def mm(a, b):
     return lax.dot_general(a, b, (((1,), (0,)), ((), ())), preferred_element_type=F32)
 
 
-def factor_diag(m_ref, B, slot):
-    for b in range(NB // B):
-        lo = b * B
-        slot(b)
-        rows = m_ref[lo:lo + B, :]
-        sub = lax.broadcasted_iota(jnp.int32, (B, 1), 0)
-        cs = [jnp.broadcast_to(rows[:, lo + j:lo + j + 1], (B, NB)) for j in range(B)]
+def wide(x):
+    return jnp.concatenate([x, x], axis=1)
+
+
+def factor_diag(m_ref, B):
+    sub = lax.broadcasted_iota(jnp.int32, (8, 1), 0)
+    T = B // 8
+
+    def tiles(x):
+        return [x[8 * t:8 * t + 8] for t in range(T)]
+
+    def row(x, s):
+        return jnp.broadcast_to(x[s:s + 1, :], x.shape)
+
+    def spread(x, j):
+        return jnp.broadcast_to(x[:, j:j + 1], (8, NB))
+
+    rows = tiles(m_ref[:B, :])
+    for lo in range(0, NB, B):
+        cs = [[spread(x, lo + j) for x in rows] for j in range(B)]
+        if lo + B < NB:
+            nxt = tiles(m_ref[lo + B:lo + 2 * B, :])
+            raw = [[spread(x, lo + j) for x in nxt] for j in range(B)]
+        done, scale = list(rows), [jnp.zeros((8, NB), F32)] * T
         for j in range(B):
-            c = cs[j]
-            r = lax.rsqrt(c[j:j + 1, :])
-            mult = jnp.where(sub > j, c * r, 0.0)
-            r2 = jnp.concatenate([r, r], axis=1)
-            pivot = rows[j:j + 1, :] * r2
-            m2 = jnp.concatenate([mult, mult], axis=1)
-            rows = jnp.where(sub == j, pivot, rows - m2 * pivot)
+            tj, sj = j // 8, j % 8
+            here = sub == sj
+            r = lax.rsqrt(row(cs[j][tj], sj))
+            half = [(jnp.where(here, 0.0, x) if t == tj else x) * r for t, x in enumerate(cs[j])]
+            q = [x * r for x in half]
+            done[tj] = jnp.where(here, rows[tj], done[tj])
+            scale[tj] = jnp.where(here, r, scale[tj])
             for i in range(j + 1, B):
-                cs[i] = cs[i] - mult * (cs[i][j:j + 1, :] * r)
-        m_ref[lo:lo + B, :] = rows
+                u = row(cs[i][tj], sj)
+                if i == j + 1:
+                    ur = u * r
+                    cs[i] = [x - y * ur for x, y in zip(cs[i], half)]
+                else:
+                    cs[i] = [x - y * u for x, y in zip(cs[i], q)]
+            p = row(rows[tj], sj)
+            rows = [x - wide(y) * p for x, y in zip(rows, q)]
+        m_ref[lo:lo + B, :] = jnp.concatenate([x * wide(y) for x, y in zip(done, scale)], axis=0)
         if lo + B < NB:
-            h, m, l = split3(rows)
-            left = jnp.concatenate([h, h, m, h, l, m], axis=0)[:, :NB]
-            right = jnp.concatenate([h, m, h, l, h, m], axis=0)
-            upd = tdot(left, right)
-            m_ref[lo + B:, :] = m_ref[lo + B:, :] - upd[lo + B:, :]
+            w = [x * wide(y * y) for x, y in zip(rows, scale)]
+            if lo + 2 * B < NB:
+                rest = m_ref[lo + 2 * B:, :]
+                h, l = split2(rest[:, :NB])
+
+                def padded(x):
+                    above = [jnp.zeros((lo, 2 * NB), BF)] if lo else []
+                    return jnp.concatenate(above + [x, jnp.zeros((NB - lo - B, 2 * NB), BF)], axis=0)
+
+                wh, wl = map(padded, split2(jnp.concatenate(w, axis=0)))
+                m_ref[lo + 2 * B:, :] = rest - mm(left3(h, l), jnp.concatenate([wh, wl, wh], axis=0))
+            rows = []
+            for t in range(T):
+                terms = [wide(raw[k][t]) * row(w[k // 8], k % 8) for k in range(B)]
+                sums = [sum(terms[g + 2:B:2], terms[g]) for g in range(2)]
+                rows.append(nxt[t] - (sums[0] + sums[1]))
 
 
 MESH = pl.DeviceIdType.MESH
@@ -122,11 +145,16 @@
         out_ref[c] = mm(pick2, jnp.concatenate(split2(x_ref[:, cols_of(c)]), axis=0))
 
     def post_rows(c):
-        def one(k, cc):
-            post(k, c, mine).start()
-            return cc
-
-        lax.fori_loop(1, fronts, one, 0)
+        for odd in (1, 0):
+            def one(t, cc):
+                k = lax.rem(2 * t + odd - mine + fronts, fronts)
+
+                @pl.when(k > 0)
+                def _():
+                    post(k, c, mine).start()
+                return cc
+
+            lax.fori_loop(0, fronts // 2, one, 0)
         in_ref[c, rows_of(mine), :] = out_ref[c, rows_of(mine), :]
 
     route(0)
@@ -251,15 +279,18 @@
 
     hold = chunks // 2
 
+    def send_block(Q, P):
+        @pl.when(Q // span == me)
+        def _():
+            o_ref[at2(Q - me * span, P)] = a_ref[at2(Q, P)]
+
+        @pl.when(Q // span != me)
+        def _():
+            ship(Q, P).start()
+
     def send_column(P):
         def one(Q, cc):
-            @pl.when(Q // span == me)
-            def _():
-                o_ref[at2(Q - me * span, P)] = a_ref[at2(Q, P)]
-
-            @pl.when(Q // span != me)
-            def _():
-                ship(Q, P).start()
+            send_block(Q, P)
             return cc
         lax.fori_loop(0, P, one, 0)
 
@@ -291,7 +322,7 @@
     def factor(p):
         m_ref[:, :NB] = a_ref[at(p, p)]
         m_ref[:, NB:] = (ri == ci).astype(F32)
-        factor_diag(m_ref, B, lambda b: None)
+        factor_diag(m_ref, B)
         a_ref[at(p, p)] = jnp.where(ci >= ri, m_ref[:, :NB], 0.0)
         return jnp.where(ci <= ri, m_ref[:, NB:], 0.0)
 
@@ -327,15 +358,16 @@
         def _():
             pl.semaphore_wait(go, 1)
 
-            def backlog(K, cc):
-                send_column(K)
-
-                @pl.when(K < P)
-                def _():
-                    send_side(K)
-                    send_pair(K)
-                return cc
-            lax.fori_loop(0, P + 1, backlog, 0)
+            def backlog(t, cc):
+                Q = side * t + (1 - side) * (P - 1 - t)
+                send_side(Q)
+                send_pair(Q)
+
+                def one(K, c3):
+                    send_block(Q, K)
+                    return c3
+                return lax.fori_loop(Q + 1, P + 1, one, cc)
+            lax.fori_loop(0, P, backlog, 0)
 
         @pl.when(P > hold)
         def _():
@@ -363,7 +395,6 @@
         keep_t(P, 0, NB, jnp.zeros((NB, NB), F32))
         mh_ref[...], ml_ref[...] = split2(dot3(rl, th, tl))
         t1 = factor(p + 1)
-        a_ref[at(p + 1, p)] = jnp.zeros((NB, NB), F32)
 
         @pl.when(P // span == me)
         def _():
@@ -391,14 +422,6 @@
             return lax.fori_loop(Q + 1, chunks, one, c)
         lax.fori_loop(lo, hi, row, 0)
 
-    def blank(i, c):
-        def one(j, cc):
-            o_ref[at2(i, j)] = jnp.zeros((CW, CW), F32)
-            return cc
-        return lax.fori_loop(0, me * span + i, one, c)
-
-    lax.fori_loop(0, span, blank, 0)
-
     @pl.when(is_root)
     def _():
         lax.fori_loop(0, chunks, supercolumn, 0)
@@ -442,7 +465,6 @@
             k = 2 * (P - me * span)
             m = rd_ref[P, :NB, :]
             o_ref[at(k, 2 * P)] = jnp.where(ci >= ri, m, 0.0)
-            o_ref[at(k + 1, 2 * P)] = jnp.zeros((NB, NB), F32)
             o_ref[at(k + 1, 2 * P + 1)] = jnp.where(ci > ri, m.T, jnp.where(ci == ri, rd_ref[P, NB:NB + 1, :], 0.0))
 
         over_blocks(me * span, me * span + span, came, came_pair)
@@ -465,7 +487,7 @@
     panels, chunks = F // NB, F // CW
     total = panels * (panels + 1) // 2
     DMA = pltpu.SemaphoreType.DMA
-    return pl.pallas_call(
+    out = pl.pallas_call(
         functools.partial(fused_body, n, fronts, cap, B),
         out_shape=jax.ShapeDtypeStruct((F // n, F), F32),
         in_specs=[pl.BlockSpec(memory_space=pltpu.VMEM)] * 5,
@@ -489,9 +511,12 @@
         ] + [pltpu.VMEM((total, NB, NB), F32)] * 3 + [pltpu.VMEM((chunks, NB + 8, NB), F32)] * 5
         + [DMA((total,))] * 2 + [DMA((chunks,))] * 2 + [DMA((chunks, chunks))] * 2 + [DMA((chunks,))] * 2 + [pltpu.SemaphoreType.REGULAR],
         compiler_params=pltpu.CompilerParams(
-            vmem_limit_bytes=60 << 20, collective_id=0, has_side_effects=True),
+            vmem_limit_bytes=(26 << 20) + 8 * (K + fronts * cap) * F, collective_id=0, has_side_effects=True),
         name="merge",
-    )(row_values, front_of_row.reshape(1, rows_held), child_factors, child_columns, damping)[None]
+    )(row_values, front_of_row.reshape(1, rows_held), child_factors, child_columns, damping)
+    held = F // n
+    below = lax.axis_index("sub") * held + lax.broadcasted_iota(jnp.int32, (held, F), 0) > lax.broadcasted_iota(jnp.int32, (held, F), 1)
+    return jnp.where(below, 0.0, out)[None]
 
 
 def solution(mesh):

time: 66.1 us -> 63.8 us (0.965)
  Pallas kernels: 63.6 us -> 59.7 us
  other arithmetic: 0 us -> 1.11 us
    pallas_call x1, Pallas kernels: 63.6 us -> 59.7 us  [local(): pl.pallas_call(functools.partial(fused_body, n, fronts, cap, B), out_shap...]
    broadcast_in_dim x0 -> x1, other arithmetic: none -> 1.11 us  [local(): return jnp.where(below, 0.0, out)[None]]
    unnamed x1 -> x10, local copies, waits for them, and re-layouts: 2.31 us -> 2.77 us
where the time goes in v3:
time: 63.8 us; the launch traced here: 63.6 us
  Pallas kernels  59.7 us (94%)
  local copies, waits for them, and re-layouts  2.77 us (4%)
  other arithmetic  1.11 us (2%)
    pallas_call x1, Pallas kernels, local(): pl.pallas_call(functools.partial(fused_body, n, fronts, cap, B), out_shap...  59.7 us
    unnamed x10, local copies, waits for them, and re-layouts  2.77 us

profile of v3, /device:TPU:16, one launch (start us, length us, event | category | flops | bytes accessed | tf_op | source)
XLA Modules:
  0.0 63.6 jit_solution(11063623185560709307)
XLA Ops:
  0.0 0.0 copy-start.3
  0.0 0.0 copy-start.2
  0.0 0.0 copy-start.4
  0.0 0.7 %copy-done.3 = f32[1,1024]{1,0:T(1,128)S(1)} copy-done((f32[1,1024]{1,0:T(1,128)S(1)}, f32[1,1024]{1,0:T(1,128)}, u32[]{:S(2)}) %copy-start.3) | copy-done | bytes 4120
  0.7 0.0 copy-done.2
  0.7 0.0 copy-done.4
  0.7 0.0 copy-start
  0.7 1.0 %copy-done = f32[128,1024]{1,0:T(8,128)S(1)} copy-done((f32[128,1024]{1,0:T(8,128)S(1)}, f32[128,1024]{1,0:T(8,128)}, u32[]{:S(2)}) %copy-start) | copy-done | bytes 524312
  1.7 0.0 copy-start.1
  1.8 1.0 %copy-done.1 = f32[2,128,512]{2,1,0:T(8,128)S(1)} copy-done((f32[2,128,512]{2,1,0:T(8,128)S(1)}, f32[2,128,512]{2,1,0:T(8,128)}, u32[]{:S(2)}) %copy-start.1) | copy-done | bytes 524312
  2.8 59.7 %merge.1 = f32[256,1024]{1,0:T(8,128)S(1)} custom-call(f32[128,1024]{1,0:T(8,128)S(1)} %copy-done, s32[1,128]{1,0:T(1,128)S(1)} %bitcast.3, f32[2,128,512]{2,1,0:T(8,128)S(1)} %copy-done.1, s32[2,512]{1,0:T(2,128)S(1)} %copy-done.2, f32[1,1024]{1,0:T(1,128)S(1)} %copy-done.3), custom_call_target="tpu_custom_call" | custom-call | tf_op jit(solution)/shard_map/merge/pallas_call | solution.py:490
  62.5 1.1 %select_bitcast_fusion = f32[1,256,1024]{2,1,0:T(8,128)} fusion(f32[256,1024]{1,0:T(8,128)S(1)} %merge.1, s32[256]{0:T(256)S(1)} %iota_add_fusion), kind=kLoop, calls=%fused_computation | loop fusion | flops 524288 | bytes 2098176 | tf_op jit(solution)/shard_map/broadcast_in_dim | solution.py:519
  (1 shorter events, 0.0 us)
Async XLA Ops:
  0.0 0.7 %copy-start.3 = (f32[1,1024]{1,0:T(1,128)S(1)}, f32[1,1024]{1,0:T(1,128)}, u32[]{:S(2)}) copy-start(f32[1,1024]{1,0:T(1,128)} %w_ref.1) | copy-start | bytes 12292
  0.0 0.7 %copy-start.2 = (s32[2,512]{1,0:T(2,128)S(1)}, s32[2,512]{1,0:T(2,128)}, u32[]{:S(2)}) copy-start(s32[2,512]{1,0:T(2,128)} %cc_ref.1) | copy-start | bytes 12292
  0.0 0.7 %copy-start.4 = (s32[128,1]{0,1:T(1,128)S(1)}, s32[128,1]{0,1:T(1,128)}, u32[]{:S(2)}) copy-start(s32[128,1]{0,1:T(1,128)} %param.6) | copy-start | bytes 1540
  0.7 1.0 %copy-start = (f32[128,1024]{1,0:T(8,128)S(1)}, f32[128,1024]{1,0:T(8,128)}, u32[]{:S(2)}) copy-start(f32[128,1024]{1,0:T(8,128)} %x_ref.1) | copy-start | bytes 1572868
  1.7 1.0 %copy-start.1 = (f32[2,128,512]{2,1,0:T(8,128)S(1)}, f32[2,128,512]{2,1,0:T(8,128)}, u32[]{:S(2)}) copy-start(f32[2,128,512]{2,1,0:T(8,128)} %ch_ref.1) | copy-start | bytes 1572868

commit v4 on v3

--- a/solution.py
+++ b/solution.py
@@ -92,9 +92,9 @@
     return jnp.concatenate([h, h, l], axis=1)
 
 
-def fused_body(n, fronts, cap, B, x_ref, d_ref, ch_ref, cc_ref, w_ref, o_ref, out_ref, in_ref, fs, fg, a_ref, m_ref, rt_ref, rr_ref, mh_ref, ml_ref, tt_ref, xh_ref, xl_ref, th_ref, tl_ref, p_ref, l_ref, f_ref, dp_ref, dl_ref, df_ref, dr_ref, rd_ref, ss, sg, ds, dg, os, og, ps, pg, go):
-    R, F = x_ref.shape
-    kids, crows, _ = ch_ref.shape
+def fused_body(n, fronts, cap, B, x_hbm, d_hbm, ch_hbm, cc_hbm, w_hbm, o_ref, x_ref, d_ref, ch_ref, cc_ref, w_ref, ls, out_ref, in_ref, fs, fg, a_ref, m_ref, rt_ref, rr_ref, mh_ref, ml_ref, tt_ref, xh_ref, xl_ref, th_ref, tl_ref, p_ref, l_ref, f_ref, dp_ref, dl_ref, df_ref, dr_ref, rd_ref, ss, sg, ds, dg, os, og, ps, pg, go):
+    R, F = x_hbm.shape
+    kids, crows, _ = ch_hbm.shape
     slots = fronts * cap
     panels = F // NB
     chunks = F // CW
@@ -132,6 +132,21 @@
             src_ref=out_ref.at[c, rows_of(to)], dst_ref=in_ref.at[c, rows_of(dst_front)], send_sem=fs.at[c, k],
             recv_sem=fg.at[c, k], device_id={"front": to}, device_id_type=MESH)
 
+    def load(c):
+        return pltpu.make_async_copy(x_hbm.at[:, cols_of(c)], x_ref.at[c], ls.at[c])
+
+    small = [pltpu.make_async_copy(src, dst, ls.at[chunks + i]) for i, (src, dst) in enumerate(
+        ((d_hbm, d_ref), (ch_hbm, ch_ref), (cc_hbm, cc_ref), (w_hbm, w_ref)))]
+    small[0].start()
+
+    def load_all(c, cc):
+        load(c).start()
+        return cc
+
+    lax.fori_loop(0, chunks, load_all, 0)
+    for copy in small[1:]:
+        copy.start()
+    small[0].wait()
     dest = d_ref[...]
     hot = dest == lax.broadcasted_iota(jnp.int32, (fronts, R), 0)
     above = lax.broadcasted_iota(jnp.int32, (R, R), 0) < lax.broadcasted_iota(jnp.int32, (R, R), 1)
@@ -142,7 +157,8 @@
     pick2 = jnp.concatenate([pick, pick], axis=1)
 
     def route(c):
-        out_ref[c] = mm(pick2, jnp.concatenate(split2(x_ref[:, cols_of(c)]), axis=0))
+        load(c).wait()
+        out_ref[c] = mm(pick2, jnp.concatenate(split2(x_ref[c]), axis=0))
 
     def post_rows(c):
         for odd in (1, 0):
@@ -167,6 +183,9 @@
         return cc
 
     lax.fori_loop(1, chunks, route_rest, 0)
+
+    for copy in small[1:]:
+        copy.wait()
 
     def place_kids(c, cc):
         for kid in range(kids):
@@ -441,20 +460,31 @@
 
     @pl.when(jnp.logical_not(is_root))
     def _():
-        def sent(c, cc):
-            hop_pair(df_ref, c).wait_send()
-            hop_block(f_ref, place(2 * c, 2 * c + 1)).wait_send()
-
+        def sent(c, lo, hi):
             def off(i, c3):
                 hop_block(f_ref, place(i, 2 * c)).wait_send()
                 hop_block(f_ref, place(i, 2 * c + 1)).wait_send()
                 return c3
-            return lax.fori_loop(0, 2 * c, off, cc)
-        lax.fori_loop(0, chunks, sent, 0)
+            lax.fori_loop(lo, hi, off, 0)
+
+        def sent_diag(c):
+            hop_pair(df_ref, c).wait_send()
+            hop_block(f_ref, place(2 * c, 2 * c + 1)).wait_send()
+
+        def whole(c, cc):
+            sent(c, 0, 2 * c)
+            sent_diag(c)
+            return cc
+
+        lax.fori_loop(0, chunks - 1, whole, 0)
+        sent(chunks - 1, 0, panels - 2 - 0)
 
         @pl.when(is_first)
         def _():
             pl.semaphore_signal(go, inc=1, device_id={"front": mine + 1 - 2 * side}, device_id_type=MESH)
+
+        sent(chunks - 1, panels - 2 - 0, panels - 2)
+        sent_diag(chunks - 1)
 
         def came(Q, P):
             ship(Q, P).wait_recv()
@@ -490,9 +520,15 @@
     out = pl.pallas_call(
         functools.partial(fused_body, n, fronts, cap, B),
         out_shape=jax.ShapeDtypeStruct((F // n, F), F32),
-        in_specs=[pl.BlockSpec(memory_space=pltpu.VMEM)] * 5,
+        in_specs=[pl.BlockSpec(memory_space=pltpu.HBM)] * 5,
         out_specs=pl.BlockSpec(memory_space=pltpu.VMEM),
         scratch_shapes=[
+            pltpu.VMEM((chunks, rows_held, CW), F32),
+            pltpu.VMEM((1, rows_held), jnp.int32),
+            pltpu.VMEM(child_factors.shape, F32),
+            pltpu.VMEM(child_columns.shape, jnp.int32),
+            pltpu.VMEM(damping.shape, F32),
+            DMA((chunks + 4,)),
             pltpu.VMEM((chunks, fronts * cap, CW), F32),
             pltpu.VMEM((chunks, fronts * cap, CW), F32),
             DMA((chunks, fronts)),
@@ -511,7 +547,7 @@
         ] + [pltpu.VMEM((total, NB, NB), F32)] * 3 + [pltpu.VMEM((chunks, NB + 8, NB), F32)] * 5
         + [DMA((total,))] * 2 + [DMA((chunks,))] * 2 + [DMA((chunks, chunks))] * 2 + [DMA((chunks,))] * 2 + [pltpu.SemaphoreType.REGULAR],
         compiler_params=pltpu.CompilerParams(
-            vmem_limit_bytes=(26 << 20) + 8 * (K + fronts * cap) * F, collective_id=0, has_side_effects=True),
+            vmem_limit_bytes=60 << 20, collective_id=0, has_side_effects=True),
         name="merge",
     )(row_values, front_of_row.reshape(1, rows_held), child_factors, child_columns, damping)
     held = F // n

time: 63.8 us -> 63.2 us (level)
  local copies, waits for them, and re-layouts: 2.77 us -> 0 us
  other arithmetic: 1.11 us -> 2.33 us
  Pallas kernels: 59.7 us -> 60.7 us
    unnamed x10 -> x0, local copies, waits for them, and re-layouts: 2.77 us -> none
    broadcast_in_dim x1, other arithmetic: 1.11 us -> 2.33 us  [local(): return jnp.where(below, 0.0, out)[None]]
    pallas_call x1, Pallas kernels: 59.7 us -> 60.7 us  [local(): pl.pallas_call(functools.partial(fused_body, n, fronts, cap, B), out_shap...]
where the time goes in v4:
time: 63.2 us; the launch traced here: 63.1 us
  Pallas kernels  60.7 us (96%)
  other arithmetic  2.33 us (4%)
    pallas_call x1, Pallas kernels, local(): pl.pallas_call(functools.partial(fused_body, n, fronts, cap, B), out_shap...  60.7 us
    broadcast_in_dim x1, other arithmetic, local(): return jnp.where(below, 0.0, out)[None]  2.33 us

profile of v4, /device:TPU:16, one launch (start us, length us, event | category | flops | bytes accessed | tf_op | source)
XLA Modules:
  0.0 63.1 jit_solution(5862378936763813554)
XLA Ops:
  0.0 60.7 %merge.1 = f32[256,1024]{1,0:T(8,128)} custom-call(f32[128,1024]{1,0:T(8,128)} %x_hbm.1, s32[1,128]{1,0:T(1,128)} %bitcast.3, f32[2,128,512]{2,1,0:T(8,128)} %ch_hbm.1, s32[2,512]{1,0:T(2,128)} %cc_hbm.1, f32[1,1024]{1,0:T(1,128)} %w_hbm.1), custom_call_target="tpu_custom_call" | custom-call | tf_op jit(solution)/shard_map/merge/pallas_call | solution.py:520
  60.7 2.3 %select_bitcast_fusion = f32[1,256,1024]{2,1,0:T(8,128)} fusion(f32[256,1024]{1,0:T(8,128)} %merge.1, s32[256]{0:T(256)S(1)} %iota_add_fusion), kind=kLoop, calls=%fused_computation | loop fusion | flops 524288 | bytes 2098176 | tf_op jit(solution)/shard_map/broadcast_in_dim | solution.py:555
  (1 shorter events, 0.0 us)

commit v5 on v4

--- a/solution.py
+++ b/solution.py
@@ -285,6 +285,9 @@
             src_ref=a_ref.at[at2(Q, P)], dst_ref=o_ref.at[at2(Q - owner * span, P)], send_sem=os.at[Q, P],
             recv_sem=og.at[Q, P], device_id={"sub": owner}, device_id_type=MESH)
 
+    def own(Q, P):
+        return pltpu.make_async_copy(a_ref.at[at2(Q, P)], o_ref.at[at2(Q - me * span, P)], os.at[Q, P])
+
     def ship_side(P):
         owner = P // span
         return pltpu.make_async_remote_copy(
@@ -301,7 +304,7 @@
     def send_block(Q, P):
         @pl.when(Q // span == me)
         def _():
-            o_ref[at2(Q - me * span, P)] = a_ref[at2(Q, P)]
+            own(Q, P).start()
 
         @pl.when(Q // span != me)
         def _():
@@ -417,7 +420,7 @@
 
         @pl.when(P // span == me)
         def _():
-            o_ref[at2(P - me * span, P)] = a_ref[at2(P, P)]
+            own(P, P).start()
 
         @pl.when(P // span != me)
         def _():
@@ -450,11 +453,19 @@
             def _():
                 ship(Q, P).wait_send()
 
+            @pl.when(Q // span == me)
+            def _():
+                own(Q, P).wait()
+
         def sent_pair(P):
             @pl.when(P // span != me)
             def _():
                 ship_side(P).wait_send()
                 ship_pair(P).wait_send()
+
+            @pl.when(P // span == me)
+            def _():
+                own(P, P).wait()
 
         over_blocks(0, chunks, sent, sent_pair)
 
@@ -494,8 +505,14 @@
             ship_pair(P).wait_recv()
             k = 2 * (P - me * span)
             m = rd_ref[P, :NB, :]
-            o_ref[at(k, 2 * P)] = jnp.where(ci >= ri, m, 0.0)
-            o_ref[at(k + 1, 2 * P + 1)] = jnp.where(ci > ri, m.T, jnp.where(ci == ri, rd_ref[P, NB:NB + 1, :], 0.0))
+            a_ref[at(2 * P, 2 * P)] = jnp.where(ci >= ri, m, 0.0)
+            a_ref[at(2 * P + 1, 2 * P + 1)] = jnp.where(ci > ri, m.T, jnp.where(ci == ri, rd_ref[P, NB:NB + 1, :], 0.0))
+            both = [pltpu.make_async_copy(a_ref.at[at(2 * P + i, 2 * P + i)], o_ref.at[at(k + i, 2 * P + i)], sem)
+                    for i, sem in enumerate((ps.at[P], os.at[P, P]))]
+            for copy in both:
+                copy.start()
+            for copy in both:
+                copy.wait()
 
         over_blocks(me * span, me * span + span, came, came_pair)
 
@@ -521,7 +538,7 @@
         functools.partial(fused_body, n, fronts, cap, B),
         out_shape=jax.ShapeDtypeStruct((F // n, F), F32),
         in_specs=[pl.BlockSpec(memory_space=pltpu.HBM)] * 5,
-        out_specs=pl.BlockSpec(memory_space=pltpu.VMEM),
+        out_specs=pl.BlockSpec(memory_space=pltpu.HBM),
         scratch_shapes=[
             pltpu.VMEM((chunks, rows_held, CW), F32),
             pltpu.VMEM((1, rows_held), jnp.int32),

time: 63.2 us -> 62.3 us (0.986)
  Pallas kernels: 60.7 us -> 59.8 us
    pallas_call x1, Pallas kernels: 60.7 us -> 59.8 us  [local(): pl.pallas_call(functools.partial(fused_body, n, fronts, cap, B), out_shap...]
where the time goes in v5:
time: 62.3 us; the launch traced here: 62.1 us
  Pallas kernels  59.8 us (96%)
  other arithmetic  2.33 us (4%)
    pallas_call x1, Pallas kernels, local(): pl.pallas_call(functools.partial(fused_body, n, fronts, cap, B), out_shap...  59.8 us
    broadcast_in_dim x1, other arithmetic, local(): return jnp.where(below, 0.0, out)[None]  2.33 us

profile of v5, /device:TPU:16, one launch (start us, length us, event | category | flops | bytes accessed | tf_op | source)
XLA Modules:
  0.0 62.1 jit_solution(4936423170792137687)
XLA Ops:
  0.0 59.8 %merge.1 = f32[256,1024]{1,0:T(8,128)} custom-call(f32[128,1024]{1,0:T(8,128)} %x_hbm.1, s32[1,128]{1,0:T(1,128)} %bitcast.3, f32[2,128,512]{2,1,0:T(8,128)} %ch_hbm.1, s32[2,512]{1,0:T(2,128)} %cc_hbm.1, f32[1,1024]{1,0:T(1,128)} %w_hbm.1), custom_call_target="tpu_custom_call" | custom-call | tf_op jit(solution)/shard_map/merge/pallas_call | solution.py:537
  59.8 2.3 %select_bitcast_fusion = f32[1,256,1024]{2,1,0:T(8,128)} fusion(f32[256,1024]{1,0:T(8,128)} %merge.1, s32[256]{0:T(256)S(1)} %iota_add_fusion), kind=kLoop, calls=%fused_computation | loop fusion | flops 524288 | bytes 2098176 | tf_op jit(solution)/shard_map/broadcast_in_dim | solution.py:572
  (1 shorter events, 0.0 us)
